TPU v7x, 32 devices: a whole 2x2x4 slice. The times are simulated.
32 devices in a mesh: tm: 4 (over y, x), users: 8 (over z, core).
Axes of the slice: x: 2, y: 2, z: 4, core: 2. Of those that a mesh axis runs over, the one named last changes fastest.
Arguments:
- features: float32 [131072, 128], P(('tm', 'users')), may hold values from -6 to 6
- home: int32 [131072, 1], P(('tm', 'users')), may hold values from 0 to 7; in each aligned block of 4096 rows (0 to 4095, 4096 to 8191, ...) at most 1024 rows name the same one
- account: int32 [131072], P(('tm', 'users')), may hold values from 0 to 127
- flags: int32 [131072], P(('tm', 'users')), may hold values 0 or 1
Outputs:
- session_mean: float32 [131072, 128], P(('tm', 'users'))
Inputs may be any that keep to these rules, and one draw needn't show every extreme that they name: `home`: the 4096 events of one device name one owner at most 1024 times, a bound that some block reaches.
All inputs are finite; a program needn't handle non-finite values. No bound on the sum of `flags` on one device may be relied on, other than what follows from the above.
Results may differ from a plain program's by a relative error of at most 0.00007.
Values sent between devices are 32-bit elements; how exact they have to be, the bound alone decides.
No kernel may reach another device: no remote copies, remote signals or barrier semaphores. Data moves between devices by JAX's collectives and lax.ppermute only.
A program may use at most 64 MiB of HBM per device.

v0:
```python
import math
import jax
import jax.numpy as jnp
from jax import lax
from jax.sharding import PartitionSpec as P

ACCOUNTS = 128
EXACT_MATMUL = lax.Precision.HIGHEST


def destination_rank(owner_of, owners):
    count_per_row = owner_of.shape[0]
    block_rows = math.gcd(count_per_row, 512)
    blocks = count_per_row // block_rows
    strict_lower = (
        lax.broadcasted_iota(jnp.int32, (block_rows, block_rows), 0)
        > lax.broadcasted_iota(jnp.int32, (block_rows, block_rows), 1)
    ).astype(jnp.float32)
    columns = jnp.arange(owners, dtype=jnp.int32)

    def destination_advance(before, block_data):
        choose_mask = (block_data[:, None] == columns[None, :]).astype(jnp.float32)
        earlier = jnp.dot(strict_lower, choose_mask, precision=EXACT_MATMUL) + before[None, :]
        return (before + jnp.sum(choose_mask, axis=0), jnp.sum(earlier * choose_mask, axis=1))

    ignored, rank_rows = lax.scan(
        destination_advance, jnp.zeros((owners,), jnp.float32), owner_of.reshape(blocks, block_rows)
    )
    return rank_rows.reshape(count_per_row).astype(jnp.int32)


def decode_rows(code_rows):
    code_ints = code_rows.astype(jnp.int32)
    is_valid = code_ints >= 0
    account_rows = jnp.where(is_valid, code_ints // 2, -1)
    flag_rows = jnp.where(is_valid, code_ints % 2, 0).astype(jnp.float32)
    return (account_rows, flag_rows)


def session_sweep(values, account_rows, flag_rows, accounts):
    count_per_row, feature_count = values.shape
    block_rows = math.gcd(count_per_row, 512)
    blocks = count_per_row // block_rows
    row_ids = lax.broadcasted_iota(jnp.int32, (block_rows, block_rows), 0)
    col_ids = lax.broadcasted_iota(jnp.int32, (block_rows, block_rows), 1)
    up_to = col_ids <= row_ids
    later_rows = col_ids > row_ids
    up_to_float = up_to.astype(jnp.float32)
    columns = jnp.arange(accounts, dtype=jnp.int32)

    def session_advance(carried, block_data):
        open_sum, open_count, already_seen = carried
        rows_values, rows_account, rows_flag = block_data
        is_live = rows_account >= 0
        indicator_matrix = (rows_account[:, None] == columns[None, :]).astype(jnp.float32)
        flag_counts = jnp.dot(
            up_to_float, indicator_matrix * rows_flag[:, None], precision=EXACT_MATMUL
        )
        own_flags = jnp.sum(flag_counts * indicator_matrix, axis=1)
        same_user = (
            (rows_account[:, None] == rows_account[None, :]) & is_live[None, :] & is_live[:, None]
        )
        same_session = (same_user & up_to & (own_flags[:, None] == own_flags[None, :])).astype(
            jnp.float32
        )
        inside_sum = jnp.dot(same_session, rows_values, precision=EXACT_MATMUL)
        inside_count = jnp.sum(same_session, axis=1)
        session_continues = jnp.where(is_live & (own_flags == 0.0), 1.0, 0.0)
        running_sum = inside_sum + session_continues[:, None] * jnp.dot(
            indicator_matrix, open_sum, precision=EXACT_MATMUL
        )
        running_count = inside_count + session_continues * jnp.dot(
            indicator_matrix, open_count, precision=EXACT_MATMUL
        )
        without_flag = session_continues * (
            1.0 - jnp.dot(indicator_matrix, already_seen, precision=EXACT_MATMUL)
        )
        followers = jnp.sum((same_user & later_rows).astype(jnp.float32), axis=1)
        last_weight = jnp.where(is_live & (followers == 0.0), 1.0, 0.0)
        present = jnp.minimum(jnp.sum(indicator_matrix, axis=0), 1.0)
        updated_sum = (
            jnp.einsum(
                "ra,rf->af",
                indicator_matrix,
                last_weight[:, None] * running_sum,
                precision=EXACT_MATMUL,
            )
            + (1.0 - present)[:, None] * open_sum
        )
        updated_count = (
            jnp.dot(last_weight * running_count, indicator_matrix, precision=EXACT_MATMUL)
            + (1.0 - present) * open_count
        )
        any_flag = jnp.minimum(jnp.sum(indicator_matrix * rows_flag[:, None], axis=0), 1.0)
        updated_seen = jnp.maximum(already_seen, any_flag)
        return (
            (updated_sum, updated_count, updated_seen),
            (running_sum, running_count, without_flag),
        )

    start_state = (
        jnp.zeros((accounts, feature_count), jnp.float32),
        jnp.zeros((accounts,), jnp.float32),
        jnp.zeros((accounts,), jnp.float32),
    )
    block_data = (
        values.reshape(blocks, block_rows, feature_count),
        account_rows.reshape(blocks, block_rows),
        flag_rows.reshape(blocks, block_rows),
    )
    closing_state, row_pieces = lax.scan(session_advance, start_state, block_data)
    running_sum = row_pieces[0].reshape(count_per_row, feature_count)
    running_count = row_pieces[1].reshape(count_per_row)
    without_flag = row_pieces[2].reshape(count_per_row)
    return (closing_state, running_sum, running_count, without_flag)


def combine_states(earlier, later):
    carry_on = 1.0 - later[2]
    return (
        later[0] + carry_on[:, None] * earlier[0],
        later[1] + carry_on * earlier[1],
        jnp.maximum(earlier[2], later[2]),
    )


def body(features, home, account, flags):
    owners = lax.axis_size("users")
    event_rows, feature_count = features.shape
    slot_cap = 2 * event_rows // owners
    accounts = ACCOUNTS
    owner_of = home[:, 0]
    rank_rows = destination_rank(owner_of, owners)
    slot_index = owner_of * slot_cap + rank_rows
    code_values = (account * 2 + flags).astype(jnp.float32)
    send_values = (
        jnp.zeros((owners * slot_cap, feature_count), jnp.float32).at[slot_index].set(features)
    )
    send_codes = jnp.full((owners * slot_cap,), -1.0, jnp.float32).at[slot_index].set(code_values)
    got_values, got_codes = (
        lax.all_to_all(
            send_values.reshape(owners, slot_cap, feature_count),
            "users",
            split_axis=0,
            concat_axis=0,
            tiled=True,
        ),
        lax.all_to_all(
            send_codes.reshape(owners, slot_cap), "users", split_axis=0, concat_axis=0, tiled=True
        ),
    )
    account_rows, flag_rows = decode_rows(got_codes.reshape(owners * slot_cap))
    closing_state, running_sum, running_count, without_flag = session_sweep(
        got_values.reshape(owners * slot_cap, feature_count), account_rows, flag_rows, accounts
    )
    identity = (
        jnp.zeros((accounts, feature_count), jnp.float32),
        jnp.zeros((accounts,), jnp.float32),
        jnp.zeros((accounts,), jnp.float32),
    )
    gathered = (
        lax.all_gather(closing_state[0], "tm", axis=0, tiled=True),
        lax.all_gather(closing_state[1], "tm", axis=0, tiled=True),
        lax.all_gather(closing_state[2], "tm", axis=0, tiled=True),
    )
    my_group = lax.axis_index("tm")
    incoming = identity
    for position in range(lax.axis_size("tm")):
        group_state = (
            gathered[0][position * accounts : (position + 1) * accounts],
            gathered[1][position * accounts : (position + 1) * accounts],
            gathered[2][position * accounts : (position + 1) * accounts],
        )
        merged = combine_states(incoming, group_state)
        incoming = (
            jnp.where(position < my_group, merged[0], incoming[0]),
            jnp.where(position < my_group, merged[1], incoming[1]),
            jnp.where(position < my_group, merged[2], incoming[2]),
        )
    columns = jnp.arange(accounts, dtype=jnp.int32)
    onehot_rows = (account_rows[:, None] == columns[None, :]).astype(jnp.float32)
    overall_sum = running_sum + without_flag[:, None] * jnp.dot(
        onehot_rows, incoming[0], precision=EXACT_MATMUL
    )
    overall_count = running_count + without_flag * jnp.dot(
        onehot_rows, incoming[1], precision=EXACT_MATMUL
    )
    session_means = overall_sum / jnp.where(overall_count > 0.0, overall_count, 1.0)[:, None]
    returned_means = lax.all_to_all(
        session_means.reshape(owners, slot_cap, feature_count),
        "users",
        split_axis=0,
        concat_axis=0,
        tiled=True,
    )
    result = returned_means.reshape(owners * slot_cap, feature_count)[slot_index]
    return result


def solution(mesh):
    return jax.shard_map(
        body,
        mesh=mesh,
        in_specs=(
            P(("tm", "users"), None),
            P(("tm", "users"), None),
            P(("tm", "users")),
            P(("tm", "users")),
        ),
        out_specs=P(("tm", "users"), None),
        check_vma=False,
    )
```

profile of v0, /device:TPU:0, one launch (start us, length us, event | category | flops | bytes accessed | tf_op | source)
XLA Modules:
  0.0 385.4 jit_solution(16359685620664613377)
XLA Ops:
  0.6 1.4 reduce.7
  2.1 5.3 %while.34 = (s32[]{:T(128)}, f32[8]{0:T(128)S(1)}, f32[8,512]{1,0:T(8,128)S(1)}, s32[8,512]{1,0:T(8,128)S(1)}, s32[]{:T(128)}, /*index=5*/s32[]{:T(128)}) while((s32[]{:T(128)}, f32[8]{0:T(128)S(1)}, f32[8,512]{1,0:T(8,128)S(1)}, s32[8,512]{1,0:T(8,128)S(1)}, s32[]{:T(128)}, /*index=5*/s32[]{:T(128)}) %tuple.69), condition=%wide.region_3.4_spmd.clone, body=%wide.region_0.3_spmd.clone.sunk | while | flops 25722380 | bytes 14623 | solution.py:26
  8.9 16.1 %scatter_custom_fusion = f32[8192]{0:T(1024)} fusion(s32[4096]{0:T(1024)S(1)} %bitcast.173, f32[4096]{0:T(1024)S(1)} %add_convert_fusion, f32[]{:T(128)} %constant.54.clone.1), kind=kCustom, calls=%fused_computation.134 | custom fusion | bytes 32772 | tf_op jit(solution)/shard_map/scatter | solution.py:139
  25.0 6.4 %all-to-all-start = ((f32[8,1,1024]{2,1,0:T(1,128)}), f32[8,1,1024]{2,1,0:T(1,128)S(1)}, u32[]{:S(2)}, u32[]{:S(2)}) async-start(f32[8,1,1024]{2,1,0:T(1,128)} %bitcast.1), calls=%async_computation | async-start | bytes 65536 | tf_op jit(solution)/shard_map/all_to_all | solution.py:148
  31.3 13.1 %scatter_custom_fusion.1 = f32[8192,128]{1,0:T(8,128)} fusion(s32[4096]{0:T(1024)S(1)} %bitcast.174, f32[4096,128]{1,0:T(8,128)} %param.8, f32[]{:T(128)} %constant.49.clone.1), kind=kCustom, calls=%fused_computation.88 | custom fusion | bytes 4194816 | tf_op jit(solution)/shard_map/scatter | solution.py:137
  44.4 5.1 %all-to-all-start.1 = ((f32[8,1024,128]{2,1,0:T(8,128)}), f32[8,1024,128]{2,1,0:T(8,128)}, u32[]{:S(2)}, u32[]{:S(2)}) async-start(f32[8,1024,128]{2,1,0:T(8,128)} %bitcast.151), calls=%async_computation.1 | async-start | bytes 8388608 | tf_op jit(solution)/shard_map/all_to_all | solution.py:141
  49.8 93.8 %all-to-all-done.1 = f32[8,1024,128]{2,1,0:T(8,128)} async-done(((f32[8,1024,128]{2,1,0:T(8,128)}), f32[8,1024,128]{2,1,0:T(8,128)}, u32[]{:S(2)}, u32[]{:S(2)}) %all-to-all-start.1) | async-done | bytes 4194336 | tf_op jit(solution)/shard_map/all_to_all | solution.py:141
  143.6 90.4 %while.35 = (s32[]{:T(128)}, f32[128,128]{1,0:T(8,128)S(1)}, f32[128]{0:T(128)S(1)}, f32[128]{0:T(128)S(1)}, f32[16,512,128]{2,1,0:T(8,128)}, /*index=5*/f32[16,...) while((s32[]{:T(128)}, f32[128,128]{1,0:T(8,128)S(1)}, ...), condition=%wide.region_12.13_spmd.clone, body=%wide.region_6.12_spmd.clone.sunk | while | flops 1016011008 | bytes 1867940 | solution.py:111
  146.0 1.7 fusion.150
  151.6 1.7 fusion.150
  157.3 1.7 fusion.150
  162.9 1.7 fusion.150
  168.6 1.7 fusion.150
  174.2 1.7 fusion.150
  179.9 1.7 fusion.150
  185.6 1.7 fusion.150
  191.2 1.7 fusion.150
  196.9 1.7 fusion.150
  202.5 1.7 fusion.150
  208.2 1.7 fusion.150
  213.8 1.7 fusion.150
  219.5 1.7 fusion.150
  225.1 1.7 fusion.150
  230.8 1.7 fusion.150
  234.0 8.0 %all-gather = f32[4,1,128]{2,1,0:T(1,128)S(1)} all-gather(f32[1,1,128]{2,1,0:T(1,128)S(1)} %bitcast.184), channel_id=1, replica_groups=mesh['tm'=4,'users'=8] {'tm'}, dimensions={0}, use_global_device_ids=true | all-gather | bytes 2560 | tf_op jit(solution)/shard_map/all_gather | solution.py:164
  242.0 7.9 %all-gather.1 = f32[4,1,128]{2,1,0:T(1,128)S(1)} all-gather(f32[1,1,128]{2,1,0:T(1,128)S(1)} %bitcast.185), channel_id=1, replica_groups=mesh['tm'=4,'users'=8] {'tm'}, dimensions={0}, use_global_device_ids=true | all-gather | bytes 2560 | tf_op jit(solution)/shard_map/all_gather | solution.py:163
  249.9 8.0 %all_gather.9 = f32[512,128]{1,0:T(8,128)S(1)} all-gather(f32[128,128]{1,0:T(8,128)S(1)} %get-tuple-element.117), channel_id=1, replica_groups=mesh['tm'=4,'users'=8] {'tm'}, dimensions={0}, use_global_device_ids=true | all-gather | bytes 327680 | tf_op jit(solution)/shard_map/all_gather | solution.py:162
  257.9 2.9 fusion.58
  260.9 9.6 %fusion.57 = f32[8192,128]{1,0:T(8,128)} fusion(f32[8192,128]{1,0:T(8,128)} %bitcast.186, f32[8192]{0:T(1024)S(1)} %compare_select_fusion.1, s32[8192]{0:T(1024)S(1)} %fusion.78, f32[8192]{0:T(1024)S(1)} %bitcast.171, f32[512,128]{1,0:T(8,128)S(1)} %all_gather.9, f32[128]{0:T(128)S(1)} %get-tuple-element.232, f32[128]{0:T(128)S(1)} %get-tuple-element.230, ...), kind=kOutput, calls=%fused_computation.83 | convolution fusion | flops 1614987264 | bytes 8751108 | tf_op jit(solution)/shard_map/dot_general | solution.py:182
  270.5 4.5 %all-to-all-start.2 = ((f32[8,1024,128]{2,1,0:T(8,128)}), f32[8,1024,128]{2,1,0:T(8,128)}, u32[]{:S(2)}, u32[]{:S(2)}) async-start(f32[8,1024,128]{2,1,0:T(8,128)} %bitcast.152), calls=%async_computation.2 | async-start | bytes 8388608 | tf_op jit(solution)/shard_map/all_to_all | solution.py:189
  275.1 94.0 %all-to-all-done.2 = f32[8,1024,128]{2,1,0:T(8,128)} async-done(((f32[8,1024,128]{2,1,0:T(8,128)}), f32[8,1024,128]{2,1,0:T(8,128)}, u32[]{:S(2)}, u32[]{:S(2)}) %all-to-all-start.2) | async-done | bytes 4194336 | tf_op jit(solution)/shard_map/all_to_all | solution.py:189
  369.0 16.4 %gather_fusion = f32[4096,128]{1,0:T(8,128)} fusion(f32[8192,128]{1,0:T(8,128)} %bitcast.19, s32[4096]{0:T(1024)S(1)} %broadcast_clamp_fusion), kind=kCustom, calls=%fused_computation | custom fusion | bytes 4210688 | tf_op jit(solution)/shard_map/gather | solution.py:196
  (305 shorter events, 69.3 us)
Async XLA Ops:
  25.0 19.5 %all-to-all-start = ((f32[8,1,1024]{2,1,0:T(1,128)}), f32[8,1,1024]{2,1,0:T(1,128)S(1)}, u32[]{:S(2)}, u32[]{:S(2)}) async-start(f32[8,1,1024]{2,1,0:T(1,128)} %bitcast.1), calls=%async_computation | async-start | bytes 65536 | tf_op jit(solution)/shard_map/all_to_all | solution.py:148
  44.4 99.2 %all-to-all-start.1 = ((f32[8,1024,128]{2,1,0:T(8,128)}), f32[8,1024,128]{2,1,0:T(8,128)}, u32[]{:S(2)}, u32[]{:S(2)}) async-start(f32[8,1024,128]{2,1,0:T(8,128)} %bitcast.151), calls=%async_computation.1 | async-start | bytes 8388608 | tf_op jit(solution)/shard_map/all_to_all | solution.py:141
  270.5 98.5 %all-to-all-start.2 = ((f32[8,1024,128]{2,1,0:T(8,128)}), f32[8,1024,128]{2,1,0:T(8,128)}, u32[]{:S(2)}, u32[]{:S(2)}) async-start(f32[8,1024,128]{2,1,0:T(8,128)} %bitcast.152), calls=%async_computation.2 | async-start | bytes 8388608 | tf_op jit(solution)/shard_map/all_to_all | solution.py:189
where the time goes:
time: 387 us; the launch traced here: 385 us
  waiting for transfers between devices  188 us (49%)
  matrix products  90.2 us (23%)
  local copies, waits for them, and re-layouts  49.7 us (13%)
  blocking collectives  23.9 us (6%)
  other arithmetic  16.1 us (4%)
  starting transfers between devices  16 us (4%)
    all_to_all x1, waiting for transfers between devices, body(): lax.all_to_all(session_means.reshape(owners, slot_cap, feature_count), 'u...  94 us
    all_to_all x1, waiting for transfers between devices, body(): lax.all_to_all(send_values.reshape(owners, slot_cap, feature_count), 'use...  93.8 us
    dot_general x16, matrix products, session_advance(): inside_sum = jnp.dot(same_session, rows_values, precision=EXACT_MATMUL)  27.3 us
    dot_general x16, matrix products, session_advance(): jnp.dot(indicator_matrix, open_sum, precision=EXACT_MATMUL)  17.8 us
    gather x1, local copies, waits for them, and re-layouts, body(): returned_means.reshape(owners * slot_cap, feature_count)[slot_index]  16.4 us
    scatter x1, local copies, waits for them, and re-layouts, body(): jnp.full((owners * slot_cap,), -1.0, jnp.float32).at[slot_index]  16.1 us
    dot_general x16, matrix products, session_advance(): jnp.dot(up_to_float, indicator_matrix * rows_flag[:, None], precision=EXA...  14.1 us
    scatter x1, local copies, waits for them, and re-layouts, body(): jnp.zeros((owners * slot_cap, feature_count), jnp.float32).at[slot_index]  13.1 us
  transfers between devices with their start and end apart: 3, of which 2 were waited for; matrix products, arithmetic and copies ran while one was open for 3% of the time, Pallas kernels for 0%

commit v1 on v0

--- a/solution.py
+++ b/solution.py
@@ -186,13 +186,21 @@
         onehot_rows, incoming[1], precision=EXACT_MATMUL
     )
     session_means = overall_sum / jnp.where(overall_count > 0.0, overall_count, 1.0)[:, None]
-    returned_means = lax.all_to_all(
-        session_means.reshape(owners, slot_cap, feature_count),
-        "users",
-        split_axis=0,
-        concat_axis=0,
-        tiled=True,
-    )
+    x = session_means.reshape(owners, slot_cap, feature_count)
+    ways, here = (lax.axis_size("users"), lax.axis_index("users"))
+    width = x.shape[0] // ways
+    shape = list(x.shape)
+    shape[0] = width
+    height = shape[0]
+    shape[0] = height * ways
+    returned_means = jnp.zeros(shape, x.dtype)
+    for mask in range(ways):
+        part = lax.dynamic_slice_in_dim(x, (here ^ mask) * width, width, axis=0)
+        if mask:
+            part = lax.ppermute(part, "users", [(d, d ^ mask) for d in range(ways)])
+        returned_means = lax.dynamic_update_slice_in_dim(
+            returned_means, part, (here ^ mask) * height, axis=0
+        )
     result = returned_means.reshape(owners * slot_cap, feature_count)[slot_index]
     return result
 

time: 387 us -> 381 us (0.984)
  the two profiles are of different devices: /device:TPU:0 before, /device:TPU:9 now
where the time goes in v1:
time: 381 us; the launch traced here: 380 us
  waiting for transfers between devices  173 us (45%)
  matrix products  85.9 us (23%)
  local copies, waits for them, and re-layouts  58.9 us (15%)
  starting transfers between devices  26.1 us (7%)
  blocking collectives  17.8 us (5%)
  other arithmetic  16.2 us (4%)
    all_to_all x1, waiting for transfers between devices, body(): lax.all_to_all(send_values.reshape(owners, slot_cap, feature_count), 'use...  90.2 us
    ppermute x7, waiting for transfers between devices, body(): part = lax.ppermute(part, 'users', [(d, d ^ mask) for d in range(ways)])  83 us
    dot_general x16, matrix products, session_advance(): inside_sum = jnp.dot(same_session, rows_values, precision=EXACT_MATMUL)  27.2 us
    dot_general x16, matrix products, session_advance(): jnp.dot(indicator_matrix, open_sum, precision=EXACT_MATMUL)  17.9 us
    gather x1, local copies, waits for them, and re-layouts, body(): returned_means.reshape(owners * slot_cap, feature_count)[slot_index]  16.4 us
    scatter x1, local copies, waits for them, and re-layouts, body(): jnp.full((owners * slot_cap,), -1.0, jnp.float32).at[slot_index]  16.1 us
    ppermute x7, starting transfers between devices, body(): part = lax.ppermute(part, 'users', [(d, d ^ mask) for d in range(ways)])  15.4 us
    dot_general x16, matrix products, session_advance(): jnp.dot(up_to_float, indicator_matrix * rows_flag[:, None], precision=EXA...  14.3 us
  transfers between devices with their start and end apart: 9, of which 6 were waited for; matrix products, arithmetic and copies ran while one was open for 5% of the time, Pallas kernels for 0%

profile of v1, /device:TPU:9, one launch (start us, length us, event | category | flops | bytes accessed | tf_op | source)
XLA Modules:
  0.0 379.6 jit_solution(17573109076530319233)
XLA Ops:
  2.1 5.3 %while.34 = (s32[]{:T(128)}, f32[8]{0:T(128)S(1)}, f32[8,512]{1,0:T(8,128)S(1)}, s32[8,512]{1,0:T(8,128)S(1)}, s32[]{:T(128)}, /*index=5*/s32[]{:T(128)}) while((s32[]{:T(128)}, f32[8]{0:T(128)S(1)}, f32[8,512]{1,0:T(8,128)S(1)}, s32[8,512]{1,0:T(8,128)S(1)}, s32[]{:T(128)}, /*index=5*/s32[]{:T(128)}) %tuple.76), condition=%wide.region_3.4_spmd.clone, body=%wide.region_0.3_spmd.clone.sunk | while | flops 25722380 | bytes 14615 | solution.py:26
  8.9 16.1 %scatter_custom_fusion = f32[8192]{0:T(1024)} fusion(s32[4096]{0:T(1024)S(1)} %bitcast.171, f32[4096]{0:T(1024)S(1)} %add_convert_fusion, f32[]{:T(128)} %constant.53.clone.1), kind=kCustom, calls=%fused_computation.135 | custom fusion | bytes 32772 | tf_op jit(solution)/shard_map/scatter | solution.py:139
  25.0 5.6 %all-to-all-start = ((f32[8,1,1024]{2,1,0:T(1,128)}), f32[8,1,1024]{2,1,0:T(1,128)S(1)}, u32[]{:S(2)}, u32[]{:S(2)}) async-start(f32[8,1,1024]{2,1,0:T(1,128)} %bitcast.1), calls=%async_computation | async-start | bytes 65536 | tf_op jit(solution)/shard_map/all_to_all | solution.py:148
  30.6 13.1 %scatter_custom_fusion.1 = f32[8192,128]{1,0:T(8,128)} fusion(s32[4096]{0:T(1024)S(1)} %bitcast.172, f32[4096,128]{1,0:T(8,128)} %param.8, f32[]{:T(128)} %constant.46.clone.1), kind=kCustom, calls=%fused_computation.88 | custom fusion | bytes 4194816 | tf_op jit(solution)/shard_map/scatter | solution.py:137
  43.7 5.1 %all-to-all-start.1 = ((f32[8,1024,128]{2,1,0:T(8,128)}), f32[8,1024,128]{2,1,0:T(8,128)}, u32[]{:S(2)}, u32[]{:S(2)}) async-start(f32[8,1024,128]{2,1,0:T(8,128)} %bitcast.149), calls=%async_computation.1 | async-start | bytes 8388608 | tf_op jit(solution)/shard_map/all_to_all | solution.py:141
  49.1 90.2 %all-to-all-done.1 = f32[8,1024,128]{2,1,0:T(8,128)} async-done(((f32[8,1024,128]{2,1,0:T(8,128)}), f32[8,1024,128]{2,1,0:T(8,128)}, u32[]{:S(2)}, u32[]{:S(2)}) %all-to-all-start.1) | async-done | bytes 4194336 | tf_op jit(solution)/shard_map/all_to_all | solution.py:141
  139.3 90.2 %while.35 = (s32[]{:T(128)}, f32[128,128]{1,0:T(8,128)S(1)}, f32[128]{0:T(128)S(1)}, f32[128]{0:T(128)S(1)}, f32[16,512,128]{2,1,0:T(8,128)}, /*index=5*/f32[16,...) while((s32[]{:T(128)}, f32[128,128]{1,0:T(8,128)S(1)}, ...), condition=%wide.region_12.13_spmd.clone, body=%wide.region_6.12_spmd.clone.sunk | while | flops 1016011008 | bytes 1868948 | solution.py:111
  146.0 1.7 fusion.150
  168.6 1.7 fusion.150
  174.2 1.7 fusion.150
  179.9 1.7 fusion.150
  185.5 1.7 fusion.150
  196.8 1.7 fusion.150
  202.5 1.7 fusion.150
  208.1 1.7 fusion.150
  219.4 1.7 fusion.150
  225.0 1.7 fusion.150
  229.5 5.9 %all-gather = f32[4,1,128]{2,1,0:T(1,128)S(1)} all-gather(f32[1,1,128]{2,1,0:T(1,128)S(1)} %bitcast.182), channel_id=1, replica_groups=mesh['tm'=4,'users'=8] {'tm'}, dimensions={0}, use_global_device_ids=true | all-gather | bytes 2560 | tf_op jit(solution)/shard_map/all_gather | solution.py:164
  235.4 5.9 %all-gather.1 = f32[4,1,128]{2,1,0:T(1,128)S(1)} all-gather(f32[1,1,128]{2,1,0:T(1,128)S(1)} %bitcast.183), channel_id=1, replica_groups=mesh['tm'=4,'users'=8] {'tm'}, dimensions={0}, use_global_device_ids=true | all-gather | bytes 2560 | tf_op jit(solution)/shard_map/all_gather | solution.py:163
  241.3 6.0 %all_gather.9 = f32[512,128]{1,0:T(8,128)S(1)} all-gather(f32[128,128]{1,0:T(8,128)S(1)} %get-tuple-element.117), channel_id=1, replica_groups=mesh['tm'=4,'users'=8] {'tm'}, dimensions={0}, use_global_device_ids=true | all-gather | bytes 327680 | tf_op jit(solution)/shard_map/all_gather | solution.py:162
  247.3 2.9 fusion.58
  250.3 5.3 %fusion.57 = f32[8192,128]{1,0:T(8,128)S(1)} fusion(f32[8192,128]{1,0:T(8,128)} %bitcast.184, f32[8192]{0:T(1024)S(1)} %compare_select_fusion.1, s32[8192]{0:T(1024)S(1)} %fusion.78, f32[8192]{0:T(1024)S(1)} %bitcast.169, f32[512,128]{1,0:T(8,128)S(1)} %all_gather.9, f32[128]{0:T(128)S(1)} %get-tuple-element.240, f32[128]{0:T(128)S(1)} %get-tuple-element.238, ...), kind=kOutput, calls=%fused_computation.83 | convolution fusion | flops 1614987264 | bytes 8751108 | tf_op jit(solution)/shard_map/dot_general | solution.py:182
  255.6 2.3 broadcast_in_dim.55
  259.0 6.5 %collective-permute-start = (f32[1,1024,128]{2,1,0:T(8,128)S(1)}, f32[1,1024,128]{2,1,0:T(8,128)S(1)}, u32[]{:S(2)}, u32[]{:S(2)}) collective-permute-start(f32[1,1024,128]{2,1,0:T(8,128)S(1)} %get-tuple-element.233), channel_id=1, source_target_pairs={{0,1},{1,0},{2,3},{3,2},{4,5},{5,4},{6,7},{7,6},{8,9},{9,8},{10,11... | collective-permute-start | bytes 1572872 | tf_op jit(solution)/shard_map/ppermute | solution.py:200
  265.5 3.2 collective-permute-start.1
  272.7 26.9 %collective-permute-done.1 = f32[1,1024,128]{2,1,0:T(8,128)S(1)} collective-permute-done((f32[1,1024,128]{2,1,0:T(8,128)S(1)}, f32[1,1024,128]{2,1,0:T(8,128)S(1)}, u32[]{:S(2)}, u32[]{:S(2)}) %collective-permute-start.1) | collective-permute-done | bytes 524320 | tf_op jit(solution)/shard_map/ppermute | solution.py:200
  299.6 2.6 collective-permute-start.6
  303.0 7.8 %collective-permute-done.2 = f32[1,1024,128]{2,1,0:T(8,128)S(1)} collective-permute-done((f32[1,1024,128]{2,1,0:T(8,128)S(1)}, f32[1,1024,128]{2,1,0:T(8,128)S(1)}, u32[]{:S(2)}, u32[]{:S(2)}) %collective-permute-start.2) | collective-permute-done | bytes 524320 | tf_op jit(solution)/shard_map/ppermute | solution.py:200
  312.5 25.0 %collective-permute-done.4 = f32[1,1024,128]{2,1,0:T(8,128)S(1)} collective-permute-done((f32[1,1024,128]{2,1,0:T(8,128)S(1)}, f32[1,1024,128]{2,1,0:T(8,128)S(1)}, u32[]{:S(2)}, u32[]{:S(2)}) %collective-permute-start.4) | collective-permute-done | bytes 524320 | tf_op jit(solution)/shard_map/ppermute | solution.py:200
  338.3 12.5 %collective-permute-done.5 = f32[1,1024,128]{2,1,0:T(8,128)S(1)} collective-permute-done((f32[1,1024,128]{2,1,0:T(8,128)S(1)}, f32[1,1024,128]{2,1,0:T(8,128)S(1)}, u32[]{:S(2)}, u32[]{:S(2)}) %collective-permute-start.5) | collective-permute-done | bytes 524320 | tf_op jit(solution)/shard_map/ppermute | solution.py:200
  351.7 10.8 %collective-permute-done.6 = f32[1,1024,128]{2,1,0:T(8,128)S(1)} collective-permute-done((f32[1,1024,128]{2,1,0:T(8,128)S(1)}, f32[1,1024,128]{2,1,0:T(8,128)S(1)}, u32[]{:S(2)}, u32[]{:S(2)}) %collective-permute-start.6) | collective-permute-done | bytes 524320 | tf_op jit(solution)/shard_map/ppermute | solution.py:200
  363.3 16.4 %gather_fusion = f32[4096,128]{1,0:T(8,128)} fusion(f32[8192,128]{1,0:T(8,128)} %bitcast.19, s32[4096]{0:T(1024)S(1)} %broadcast_clamp_fusion), kind=kCustom, calls=%fused_computation | custom fusion | bytes 4210688 | tf_op jit(solution)/shard_map/gather | solution.py:204
  (326 shorter events, 91.1 us)
Async XLA Ops:
  25.0 18.7 %all-to-all-start = ((f32[8,1,1024]{2,1,0:T(1,128)}), f32[8,1,1024]{2,1,0:T(1,128)S(1)}, u32[]{:S(2)}, u32[]{:S(2)}) async-start(f32[8,1,1024]{2,1,0:T(1,128)} %bitcast.1), calls=%async_computation | async-start | bytes 65536 | tf_op jit(solution)/shard_map/all_to_all | solution.py:148
  43.7 95.6 %all-to-all-start.1 = ((f32[8,1024,128]{2,1,0:T(8,128)}), f32[8,1024,128]{2,1,0:T(8,128)}, u32[]{:S(2)}, u32[]{:S(2)}) async-start(f32[8,1024,128]{2,1,0:T(8,128)} %bitcast.149), calls=%async_computation.1 | async-start | bytes 8388608 | tf_op jit(solution)/shard_map/all_to_all | solution.py:141
  259.0 12.7 %collective-permute-start = (f32[1,1024,128]{2,1,0:T(8,128)S(1)}, f32[1,1024,128]{2,1,0:T(8,128)S(1)}, u32[]{:S(2)}, u32[]{:S(2)}) collective-permute-start(f32[1,1024,128]{2,1,0:T(8,128)S(1)} %get-tuple-element.233), channel_id=1, source_target_pairs={{0,1},{1,0},{2,3},{3,2},{4,5},{5,4},{6,7},{7,6},{8,9},{9,8},{10,11... | collective-permute-start | bytes 1572872 | tf_op jit(solution)/shard_map/ppermute | solution.py:200
  265.5 34.1 %collective-permute-start.1 = (f32[1,1024,128]{2,1,0:T(8,128)S(1)}, f32[1,1024,128]{2,1,0:T(8,128)S(1)}, u32[]{:S(2)}, u32[]{:S(2)}) collective-permute-start(f32[1,1024,128]{2,1,0:T(8,128)S(1)} %get-tuple-element.232), channel_id=1, source_target_pairs={{0,2},{1,3},{2,0},{3,1},{4,6},{5,7},{6,4},{7,5},{8,10},{9,11},{10,... | collective-permute-start | bytes 1572872 | tf_op jit(solution)/shard_map/ppermute | solution.py:200
  268.7 42.1 %collective-permute-start.2 = (f32[1,1024,128]{2,1,0:T(8,128)S(1)}, f32[1,1024,128]{2,1,0:T(8,128)S(1)}, u32[]{:S(2)}, u32[]{:S(2)}) collective-permute-start(f32[1,1024,128]{2,1,0:T(8,128)S(1)} %get-tuple-element.231), channel_id=1, source_target_pairs={{0,3},{1,2},{2,1},{3,0},{4,7},{5,6},{6,5},{7,4},{8,11},{9,10},{10,... | collective-permute-start | bytes 1572872 | tf_op jit(solution)/shard_map/ppermute | solution.py:200
  268.7 42.9 %collective-permute-start.3 = (f32[1,1024,128]{2,1,0:T(8,128)S(1)}, f32[1,1024,128]{2,1,0:T(8,128)S(1)}, u32[]{:S(2)}, u32[]{:S(2)}) collective-permute-start(f32[1,1024,128]{2,1,0:T(8,128)S(1)} %get-tuple-element.230), channel_id=1, source_target_pairs={{0,4},{1,5},{2,6},{3,7},{4,0},{5,1},{6,2},{7,3},{8,12},{9,13},{10,... | collective-permute-start | bytes 1572872 | tf_op jit(solution)/shard_map/ppermute | solution.py:200
  270.2 67.3 %collective-permute-start.4 = (f32[1,1024,128]{2,1,0:T(8,128)S(1)}, f32[1,1024,128]{2,1,0:T(8,128)S(1)}, u32[]{:S(2)}, u32[]{:S(2)}) collective-permute-start(f32[1,1024,128]{2,1,0:T(8,128)S(1)} %get-tuple-element.229), channel_id=1, source_target_pairs={{0,5},{1,4},{2,7},{3,6},{4,1},{5,0},{6,3},{7,2},{8,13},{9,12},{10,... | collective-permute-start | bytes 1572872 | tf_op jit(solution)/shard_map/ppermute | solution.py:200
  271.7 79.1 %collective-permute-start.5 = (f32[1,1024,128]{2,1,0:T(8,128)S(1)}, f32[1,1024,128]{2,1,0:T(8,128)S(1)}, u32[]{:S(2)}, u32[]{:S(2)}) collective-permute-start(f32[1,1024,128]{2,1,0:T(8,128)S(1)} %get-tuple-element.228), channel_id=1, source_target_pairs={{0,6},{1,7},{2,4},{3,5},{4,2},{5,3},{6,0},{7,1},{8,14},{9,15},{10,... | collective-permute-start | bytes 1572872 | tf_op jit(solution)/shard_map/ppermute | solution.py:200
  299.6 62.9 %collective-permute-start.6 = (f32[1,1024,128]{2,1,0:T(8,128)S(1)}, f32[1,1024,128]{2,1,0:T(8,128)S(1)}, u32[]{:S(2)}, u32[]{:S(2)}) collective-permute-start(f32[1,1024,128]{2,1,0:T(8,128)S(1)} %get-tuple-element.227), channel_id=1, source_target_pairs={{0,7},{1,6},{2,5},{3,4},{4,3},{5,2},{6,1},{7,0},{8,15},{9,14},{10,... | collective-permute-start | bytes 1572872 | tf_op jit(solution)/shard_map/ppermute | solution.py:200
